TPU v7x, 32 devices: a whole 2x2x4 slice. The times are simulated.
32 devices in a mesh: blk: 16 (over z, y, core), rows: 2 (over x).
Axes of the slice: x: 2, y: 2, z: 4, core: 2. Of those that a mesh axis runs over, the one named last changes fastest.
Arguments:
- columns: float32 [2048, 1280], P('blk', 'rows'), may hold values from -9 to 9
- right_factor: float32 [2048, 512], P('blk', 'rows'), may hold values from -6 to 6
Outputs:
- new_columns: float32 [2048, 1280], P('blk', 'rows')
- new_factor: float32 [2048, 512], P('blk', 'rows')
All inputs are finite; a program needn't handle non-finite values.
Results may differ from a plain program's by a relative error of at most 0.0003.
Values sent between devices are 32-bit elements; how exact they have to be, the bound alone decides.
A program may use at most 64 MiB of HBM per device.

v0:
```python
import jax
import jax.numpy as jnp
from jax import lax
from jax.sharding import PartitionSpec as P

STEPS = 6
HIGHEST_PREC = lax.Precision.HIGHEST


def shifted(block, axis, distance):
    devices = range(lax.axis_size(axis))
    route = [((i - distance) % len(devices), i) for i in devices]
    return lax.ppermute(block, axis, route)


def rotation(pair_gram):
    first = jnp.linalg.cholesky(jnp.dot(pair_gram, pair_gram, precision=HIGHEST_PREC))
    second = jnp.linalg.cholesky(jnp.dot(first.T, first, precision=HIGHEST_PREC))
    return jax.scipy.linalg.solve_triangular(second, first.T, lower=True).T


def gram_of(upper_rows, lower_rows):
    return lax.dot_general(upper_rows, lower_rows, (((1,), (1,)), ((), ())), precision=HIGHEST_PREC)


def rotate(rotation_matrix, blocks):
    return lax.dot_general(
        rotation_matrix, blocks, (((0,), (0,)), ((), ())), precision=HIGHEST_PREC
    )


def body(columns, right_factor):
    block_width = columns.shape[0] // 2
    stay_gram, moving_gram = lax.psum(
        (
            gram_of(columns[:block_width], columns[:block_width]),
            gram_of(columns[block_width:], columns[block_width:]),
        ),
        "rows",
    )

    def advance_cross(step_index, loop_state):
        column_pair, factor_pair, stay_gram, moving_gram = loop_state
        cross_term = lax.psum(gram_of(column_pair[:block_width], column_pair[block_width:]), "rows")
        upper_half = jnp.concatenate([stay_gram, cross_term], 1)
        lower_half = jnp.concatenate([cross_term.T, moving_gram], 1)
        pair_gram = jnp.concatenate([upper_half, lower_half], 0)
        rotation_matrix = rotation(pair_gram)
        column_pair = rotate(rotation_matrix, column_pair)
        factor_pair = rotate(rotation_matrix, factor_pair)
        rotated_gram = rotate(
            rotation_matrix, jnp.dot(pair_gram, rotation_matrix, precision=HIGHEST_PREC)
        )
        arrived = shifted(
            (
                column_pair[block_width:],
                factor_pair[block_width:],
                rotated_gram[block_width:, block_width:],
            ),
            "blk",
            1,
        )
        return (
            jnp.concatenate([column_pair[:block_width], arrived[0]], 0),
            jnp.concatenate([factor_pair[:block_width], arrived[1]], 0),
            rotated_gram[:block_width, :block_width],
            arrived[2],
        )

    result = lax.fori_loop(0, STEPS, advance_cross, (columns, right_factor, stay_gram, moving_gram))
    return (result[0], result[1])


def solution(mesh):
    return jax.shard_map(
        body,
        mesh=mesh,
        in_specs=(P("blk", "rows"), P("blk", "rows")),
        out_specs=(P("blk", "rows"), P("blk", "rows")),
        check_vma=False,
    )
```

profile of v0, /device:TPU:0, one launch (start us, length us, event | category | flops | bytes accessed | tf_op | source)
XLA Modules:
  0.0 344.3 jit_solution(13452265809952207676)
XLA Ops:
  0.6 1.0 copy.37
  2.2 10.4 %all-reduce = (f32[64,64]{1,0:T(8,128)S(1)}, f32[64,64]{1,0:T(8,128)S(1)}) all-reduce(f32[64,64]{1,0:T(8,128)S(1)} %fusion.27, f32[64,64]{1,0:T(8,128)S(1)} %fusion.25), channel_id=1, replica_groups=mesh['blk'=16,'rows'=2] {'rows'}, use_global_device_ids=true, to_apply=%region_0.0 | all-reduce | flops 8192 | bytes 65536 | tf_op jit(solution)/shard_map/psum | solution.py:34
  12.7 330.9 %while.16 = (s32[]{:T(128)}, f32[128,640]{1,0:T(8,128)S(1)}, f32[128,256]{1,0:T(8,128)S(1)}, f32[64,64]{1,0:T(8,128)S(1)}, f32[64,64]{1,0:T(8,128)S(1)}, /*index=5*/s32[]{:T(128)}) while((s32[]{:T(128)}, f32[128,640]{1,0:T(8,128)S(1)}, f32[128,256]{1,0:T(8,128)S(1)}, f32[64,64]{1,0:T(8,128)S(1)}, f32[64,64]{1,0:T(8,128)S(1)}, ...), condition=%wide.region_6.8_spmd, body=%wide.region_2.7_spmd.sunk | while | flops 333992192 | bytes 6179010 | solution.py:70
  13.2 6.9 %psum.24 = f32[64,64]{1,0:T(8,128)S(1)} all-reduce(f32[64,64]{1,0:T(8,128)S(1)} %fusion.77), channel_id=1, replica_groups=mesh['blk'=16,'rows'=2] {'rows'}, use_global_device_ids=true, to_apply=%region_3.0 | all-reduce | flops 4096 | bytes 32768 | tf_op jit(solution)/shard_map/while/body/eval_jaxpr/psum | solution.py:44
  20.7 11.7 %cholesky.175 = f32[128,128]{1,0:T(8,128)S(1)} custom-call(f32[128,128]{1,0:T(8,128)S(1)} %fusion.79), custom_call_target="Cholesky" | custom-call | tf_op jit(solution)/shard_map/while/body/eval_jaxpr/jit(cholesky)/cholesky | solution.py:17
  33.0 0.9 fusion.81
  34.1 11.7 %cholesky.176 = f32[128,128]{1,0:T(8,128)S(1)} custom-call(f32[128,128]{1,0:T(8,128)S(1)} %fusion.82), custom_call_target="Cholesky" | custom-call | tf_op jit(solution)/shard_map/while/body/eval_jaxpr/jit(cholesky)/cholesky | solution.py:18
  45.8 0.7 compare_reduce_fusion.5
  46.6 0.7 fusion.83
  47.3 9.8 %custom-call.7 = f32[1,128,128]{1,2,0:T(8,128)S(1)} custom-call(f32[1,128,128]{2,1,0:T(8,128)S(1)} %fusion.83), custom_call_target="InvertDiagBlocksLowerTriangular" | custom-call | tf_op jit(solution)/shard_map/while/body/eval_jaxpr/jit(_solve_triangular)/triangular_solve | solution.py:19
  57.1 0.9 fusion.84
  58.8 2.0 collective-permute-start
  61.5 3.2 collective-permute-done.1
  64.8 1.7 collective-permute-done
  66.5 1.0 collective-permute-done.2
  68.0 8.3 %psum.24 = f32[64,64]{1,0:T(8,128)S(1)} all-reduce(f32[64,64]{1,0:T(8,128)S(1)} %fusion.77), channel_id=1, replica_groups=mesh['blk'=16,'rows'=2] {'rows'}, use_global_device_ids=true, to_apply=%region_3.0 | all-reduce | flops 4096 | bytes 32768 | tf_op jit(solution)/shard_map/while/body/eval_jaxpr/psum | solution.py:44
  76.9 11.7 %cholesky.175 = f32[128,128]{1,0:T(8,128)S(1)} custom-call(f32[128,128]{1,0:T(8,128)S(1)} %fusion.79), custom_call_target="Cholesky" | custom-call | tf_op jit(solution)/shard_map/while/body/eval_jaxpr/jit(cholesky)/cholesky | solution.py:17
  89.3 0.9 fusion.81
  90.4 11.7 %cholesky.176 = f32[128,128]{1,0:T(8,128)S(1)} custom-call(f32[128,128]{1,0:T(8,128)S(1)} %fusion.82), custom_call_target="Cholesky" | custom-call | tf_op jit(solution)/shard_map/while/body/eval_jaxpr/jit(cholesky)/cholesky | solution.py:18
  102.1 0.7 compare_reduce_fusion.5
  102.8 0.7 fusion.83
  103.5 9.8 %custom-call.7 = f32[1,128,128]{1,2,0:T(8,128)S(1)} custom-call(f32[1,128,128]{2,1,0:T(8,128)S(1)} %fusion.83), custom_call_target="InvertDiagBlocksLowerTriangular" | custom-call | tf_op jit(solution)/shard_map/while/body/eval_jaxpr/jit(_solve_triangular)/triangular_solve | solution.py:19
  113.3 0.9 fusion.84
  115.8 5.2 %collective-permute-done.1 = f32[64,256]{1,0:T(8,128)S(1)} collective-permute-done((f32[64,256]{1,0:T(8,128)S(1)}, f32[64,256]{1,0:T(8,128)S(1)}, u32[]{:S(2)}, u32[]{:S(2)}) %collective-permute-start.1) | collective-permute-done | bytes 65568 | tf_op jit(solution)/shard_map/while/body/eval_jaxpr/ppermute | solution.py:13
  121.0 1.7 collective-permute-done
  123.6 7.4 %psum.24 = f32[64,64]{1,0:T(8,128)S(1)} all-reduce(f32[64,64]{1,0:T(8,128)S(1)} %fusion.77), channel_id=1, replica_groups=mesh['blk'=16,'rows'=2] {'rows'}, use_global_device_ids=true, to_apply=%region_3.0 | all-reduce | flops 4096 | bytes 32768 | tf_op jit(solution)/shard_map/while/body/eval_jaxpr/psum | solution.py:44
  131.6 11.7 %cholesky.175 = f32[128,128]{1,0:T(8,128)S(1)} custom-call(f32[128,128]{1,0:T(8,128)S(1)} %fusion.79), custom_call_target="Cholesky" | custom-call | tf_op jit(solution)/shard_map/while/body/eval_jaxpr/jit(cholesky)/cholesky | solution.py:17
  143.9 0.9 fusion.81
  145.0 11.7 %cholesky.176 = f32[128,128]{1,0:T(8,128)S(1)} custom-call(f32[128,128]{1,0:T(8,128)S(1)} %fusion.82), custom_call_target="Cholesky" | custom-call | tf_op jit(solution)/shard_map/while/body/eval_jaxpr/jit(cholesky)/cholesky | solution.py:18
  156.7 0.7 compare_reduce_fusion.5
  157.5 0.7 fusion.83
  158.2 9.8 %custom-call.7 = f32[1,128,128]{1,2,0:T(8,128)S(1)} custom-call(f32[1,128,128]{2,1,0:T(8,128)S(1)} %fusion.83), custom_call_target="InvertDiagBlocksLowerTriangular" | custom-call | tf_op jit(solution)/shard_map/while/body/eval_jaxpr/jit(_solve_triangular)/triangular_solve | solution.py:19
  168.0 0.9 fusion.84
  170.5 5.2 %collective-permute-done.1 = f32[64,256]{1,0:T(8,128)S(1)} collective-permute-done((f32[64,256]{1,0:T(8,128)S(1)}, f32[64,256]{1,0:T(8,128)S(1)}, u32[]{:S(2)}, u32[]{:S(2)}) %collective-permute-start.1) | collective-permute-done | bytes 65568 | tf_op jit(solution)/shard_map/while/body/eval_jaxpr/ppermute | solution.py:13
  175.7 1.7 collective-permute-done
  178.2 8.3 %psum.24 = f32[64,64]{1,0:T(8,128)S(1)} all-reduce(f32[64,64]{1,0:T(8,128)S(1)} %fusion.77), channel_id=1, replica_groups=mesh['blk'=16,'rows'=2] {'rows'}, use_global_device_ids=true, to_apply=%region_3.0 | all-reduce | flops 4096 | bytes 32768 | tf_op jit(solution)/shard_map/while/body/eval_jaxpr/psum | solution.py:44
  187.1 11.7 %cholesky.175 = f32[128,128]{1,0:T(8,128)S(1)} custom-call(f32[128,128]{1,0:T(8,128)S(1)} %fusion.79), custom_call_target="Cholesky" | custom-call | tf_op jit(solution)/shard_map/while/body/eval_jaxpr/jit(cholesky)/cholesky | solution.py:17
  199.5 0.9 fusion.81
  200.6 11.7 %cholesky.176 = f32[128,128]{1,0:T(8,128)S(1)} custom-call(f32[128,128]{1,0:T(8,128)S(1)} %fusion.82), custom_call_target="Cholesky" | custom-call | tf_op jit(solution)/shard_map/while/body/eval_jaxpr/jit(cholesky)/cholesky | solution.py:18
  212.3 0.7 compare_reduce_fusion.5
  213.0 0.7 fusion.83
  213.8 9.8 %custom-call.7 = f32[1,128,128]{1,2,0:T(8,128)S(1)} custom-call(f32[1,128,128]{2,1,0:T(8,128)S(1)} %fusion.83), custom_call_target="InvertDiagBlocksLowerTriangular" | custom-call | tf_op jit(solution)/shard_map/while/body/eval_jaxpr/jit(_solve_triangular)/triangular_solve | solution.py:19
  223.6 0.9 fusion.84
  226.0 5.2 %collective-permute-done.1 = f32[64,256]{1,0:T(8,128)S(1)} collective-permute-done((f32[64,256]{1,0:T(8,128)S(1)}, f32[64,256]{1,0:T(8,128)S(1)}, u32[]{:S(2)}, u32[]{:S(2)}) %collective-permute-start.1) | collective-permute-done | bytes 65568 | tf_op jit(solution)/shard_map/while/body/eval_jaxpr/ppermute | solution.py:13
  231.3 1.7 collective-permute-done
  233.8 7.4 %psum.24 = f32[64,64]{1,0:T(8,128)S(1)} all-reduce(f32[64,64]{1,0:T(8,128)S(1)} %fusion.77), channel_id=1, replica_groups=mesh['blk'=16,'rows'=2] {'rows'}, use_global_device_ids=true, to_apply=%region_3.0 | all-reduce | flops 4096 | bytes 32768 | tf_op jit(solution)/shard_map/while/body/eval_jaxpr/psum | solution.py:44
  241.8 11.7 %cholesky.175 = f32[128,128]{1,0:T(8,128)S(1)} custom-call(f32[128,128]{1,0:T(8,128)S(1)} %fusion.79), custom_call_target="Cholesky" | custom-call | tf_op jit(solution)/shard_map/while/body/eval_jaxpr/jit(cholesky)/cholesky | solution.py:17
  254.2 0.9 fusion.81
  255.2 11.7 %cholesky.176 = f32[128,128]{1,0:T(8,128)S(1)} custom-call(f32[128,128]{1,0:T(8,128)S(1)} %fusion.82), custom_call_target="Cholesky" | custom-call | tf_op jit(solution)/shard_map/while/body/eval_jaxpr/jit(cholesky)/cholesky | solution.py:18
  267.0 0.7 compare_reduce_fusion.5
  268.4 9.8 %custom-call.7 = f32[1,128,128]{1,2,0:T(8,128)S(1)} custom-call(f32[1,128,128]{2,1,0:T(8,128)S(1)} %fusion.83), custom_call_target="InvertDiagBlocksLowerTriangular" | custom-call | tf_op jit(solution)/shard_map/while/body/eval_jaxpr/jit(_solve_triangular)/triangular_solve | solution.py:19
  278.2 0.9 fusion.84
  280.7 5.2 %collective-permute-done.1 = f32[64,256]{1,0:T(8,128)S(1)} collective-permute-done((f32[64,256]{1,0:T(8,128)S(1)}, f32[64,256]{1,0:T(8,128)S(1)}, u32[]{:S(2)}, u32[]{:S(2)}) %collective-permute-start.1) | collective-permute-done | bytes 65568 | tf_op jit(solution)/shard_map/while/body/eval_jaxpr/ppermute | solution.py:13
  285.9 1.7 collective-permute-done
  288.5 8.3 %psum.24 = f32[64,64]{1,0:T(8,128)S(1)} all-reduce(f32[64,64]{1,0:T(8,128)S(1)} %fusion.77), channel_id=1, replica_groups=mesh['blk'=16,'rows'=2] {'rows'}, use_global_device_ids=true, to_apply=%region_3.0 | all-reduce | flops 4096 | bytes 32768 | tf_op jit(solution)/shard_map/while/body/eval_jaxpr/psum | solution.py:44
  297.4 11.7 %cholesky.175 = f32[128,128]{1,0:T(8,128)S(1)} custom-call(f32[128,128]{1,0:T(8,128)S(1)} %fusion.79), custom_call_target="Cholesky" | custom-call | tf_op jit(solution)/shard_map/while/body/eval_jaxpr/jit(cholesky)/cholesky | solution.py:17
  309.8 0.9 fusion.81
  310.8 11.7 %cholesky.176 = f32[128,128]{1,0:T(8,128)S(1)} custom-call(f32[128,128]{1,0:T(8,128)S(1)} %fusion.82), custom_call_target="Cholesky" | custom-call | tf_op jit(solution)/shard_map/while/body/eval_jaxpr/jit(cholesky)/cholesky | solution.py:18
  322.6 0.7 compare_reduce_fusion.5
  324.0 9.8 %custom-call.7 = f32[1,128,128]{1,2,0:T(8,128)S(1)} custom-call(f32[1,128,128]{2,1,0:T(8,128)S(1)} %fusion.83), custom_call_target="InvertDiagBlocksLowerTriangular" | custom-call | tf_op jit(solution)/shard_map/while/body/eval_jaxpr/jit(_solve_triangular)/triangular_solve | solution.py:19
  333.8 0.9 fusion.84
  336.3 5.2 %collective-permute-done.1 = f32[64,256]{1,0:T(8,128)S(1)} collective-permute-done((f32[64,256]{1,0:T(8,128)S(1)}, f32[64,256]{1,0:T(8,128)S(1)}, u32[]{:S(2)}, u32[]{:S(2)}) %collective-permute-start.1) | collective-permute-done | bytes 65568 | tf_op jit(solution)/shard_map/while/body/eval_jaxpr/ppermute | solution.py:13
  341.5 1.7 collective-permute-done
  343.6 0.7 copy-done
  (157 shorter events, 23.6 us)
Async XLA Ops:
  1.9 10.8 %copy-start.2 = (f32[128,256]{1,0:T(8,128)S(1)}, f32[128,256]{1,0:T(8,128)}, u32[]{:S(2)}) copy-start(f32[128,256]{1,0:T(8,128)} %param.6) | copy-start | bytes 393220
  58.3 6.4 %collective-permute-start.1 = (f32[64,256]{1,0:T(8,128)S(1)}, f32[64,256]{1,0:T(8,128)S(1)}, u32[]{:S(2)}, u32[]{:S(2)}) collective-permute-start(f32[64,256]{1,0:T(8,128)S(1)} %get-tuple-element.90), channel_id=1, source_target_pairs={{30,0},{0,2},{2,4},{4,6},{6,8},{8,10},{10,12},{12,14},{14,16},{16,... | collective-permute-start | bytes 196616 | tf_op jit(solution)/shard_map/while/body/eval_jaxpr/ppermute | solution.py:13
  58.8 7.7 %collective-permute-start = (f32[64,640]{1,0:T(8,128)S(1)}, f32[64,640]{1,0:T(8,128)S(1)}, u32[]{:S(2)}, u32[]{:S(2)}) collective-permute-start(f32[64,640]{1,0:T(8,128)S(1)} %get-tuple-element.88), channel_id=1, source_target_pairs={{30,0},{0,2},{2,4},{4,6},{6,8},{8,10},{10,12},{12,14},{14,16},{16,... | collective-permute-start | bytes 491528 | tf_op jit(solution)/shard_map/while/body/eval_jaxpr/ppermute | solution.py:13
  61.5 6.0 %collective-permute-start.2 = (f32[64,64]{1,0:T(8,128)S(1)}, f32[64,64]{1,0:T(8,128)S(1)}, u32[]{:S(2)}, u32[]{:S(2)}) collective-permute-start(f32[64,64]{1,0:T(8,128)S(1)} %get-tuple-element.93), channel_id=1, source_target_pairs={{30,0},{0,2},{2,4},{4,6},{6,8},{8,10},{10,12},{12,14},{14,16},{16,... | collective-permute-start | bytes 49160 | tf_op jit(solution)/shard_map/while/body/eval_jaxpr/ppermute | solution.py:13
  114.6 6.4 %collective-permute-start.1 = (f32[64,256]{1,0:T(8,128)S(1)}, f32[64,256]{1,0:T(8,128)S(1)}, u32[]{:S(2)}, u32[]{:S(2)}) collective-permute-start(f32[64,256]{1,0:T(8,128)S(1)} %get-tuple-element.90), channel_id=1, source_target_pairs={{30,0},{0,2},{2,4},{4,6},{6,8},{8,10},{10,12},{12,14},{14,16},{16,... | collective-permute-start | bytes 196616 | tf_op jit(solution)/shard_map/while/body/eval_jaxpr/ppermute | solution.py:13
  115.1 7.7 %collective-permute-start = (f32[64,640]{1,0:T(8,128)S(1)}, f32[64,640]{1,0:T(8,128)S(1)}, u32[]{:S(2)}, u32[]{:S(2)}) collective-permute-start(f32[64,640]{1,0:T(8,128)S(1)} %get-tuple-element.88), channel_id=1, source_target_pairs={{30,0},{0,2},{2,4},{4,6},{6,8},{8,10},{10,12},{12,14},{14,16},{16,... | collective-permute-start | bytes 491528 | tf_op jit(solution)/shard_map/while/body/eval_jaxpr/ppermute | solution.py:13
  115.8 7.3 %collective-permute-start.2 = (f32[64,64]{1,0:T(8,128)S(1)}, f32[64,64]{1,0:T(8,128)S(1)}, u32[]{:S(2)}, u32[]{:S(2)}) collective-permute-start(f32[64,64]{1,0:T(8,128)S(1)} %get-tuple-element.93), channel_id=1, source_target_pairs={{30,0},{0,2},{2,4},{4,6},{6,8},{8,10},{10,12},{12,14},{14,16},{16,... | collective-permute-start | bytes 49160 | tf_op jit(solution)/shard_map/while/body/eval_jaxpr/ppermute | solution.py:13
  169.2 6.4 %collective-permute-start.1 = (f32[64,256]{1,0:T(8,128)S(1)}, f32[64,256]{1,0:T(8,128)S(1)}, u32[]{:S(2)}, u32[]{:S(2)}) collective-permute-start(f32[64,256]{1,0:T(8,128)S(1)} %get-tuple-element.90), channel_id=1, source_target_pairs={{30,0},{0,2},{2,4},{4,6},{6,8},{8,10},{10,12},{12,14},{14,16},{16,... | collective-permute-start | bytes 196616 | tf_op jit(solution)/shard_map/while/body/eval_jaxpr/ppermute | solution.py:13
  169.7 7.7 %collective-permute-start = (f32[64,640]{1,0:T(8,128)S(1)}, f32[64,640]{1,0:T(8,128)S(1)}, u32[]{:S(2)}, u32[]{:S(2)}) collective-permute-start(f32[64,640]{1,0:T(8,128)S(1)} %get-tuple-element.88), channel_id=1, source_target_pairs={{30,0},{0,2},{2,4},{4,6},{6,8},{8,10},{10,12},{12,14},{14,16},{16,... | collective-permute-start | bytes 491528 | tf_op jit(solution)/shard_map/while/body/eval_jaxpr/ppermute | solution.py:13
  170.4 7.3 %collective-permute-start.2 = (f32[64,64]{1,0:T(8,128)S(1)}, f32[64,64]{1,0:T(8,128)S(1)}, u32[]{:S(2)}, u32[]{:S(2)}) collective-permute-start(f32[64,64]{1,0:T(8,128)S(1)} %get-tuple-element.93), channel_id=1, source_target_pairs={{30,0},{0,2},{2,4},{4,6},{6,8},{8,10},{10,12},{12,14},{14,16},{16,... | collective-permute-start | bytes 49160 | tf_op jit(solution)/shard_map/while/body/eval_jaxpr/ppermute | solution.py:13
  224.8 6.4 %collective-permute-start.1 = (f32[64,256]{1,0:T(8,128)S(1)}, f32[64,256]{1,0:T(8,128)S(1)}, u32[]{:S(2)}, u32[]{:S(2)}) collective-permute-start(f32[64,256]{1,0:T(8,128)S(1)} %get-tuple-element.90), channel_id=1, source_target_pairs={{30,0},{0,2},{2,4},{4,6},{6,8},{8,10},{10,12},{12,14},{14,16},{16,... | collective-permute-start | bytes 196616 | tf_op jit(solution)/shard_map/while/body/eval_jaxpr/ppermute | solution.py:13
  225.3 7.7 %collective-permute-start = (f32[64,640]{1,0:T(8,128)S(1)}, f32[64,640]{1,0:T(8,128)S(1)}, u32[]{:S(2)}, u32[]{:S(2)}) collective-permute-start(f32[64,640]{1,0:T(8,128)S(1)} %get-tuple-element.88), channel_id=1, source_target_pairs={{30,0},{0,2},{2,4},{4,6},{6,8},{8,10},{10,12},{12,14},{14,16},{16,... | collective-permute-start | bytes 491528 | tf_op jit(solution)/shard_map/while/body/eval_jaxpr/ppermute | solution.py:13
  226.0 7.3 %collective-permute-start.2 = (f32[64,64]{1,0:T(8,128)S(1)}, f32[64,64]{1,0:T(8,128)S(1)}, u32[]{:S(2)}, u32[]{:S(2)}) collective-permute-start(f32[64,64]{1,0:T(8,128)S(1)} %get-tuple-element.93), channel_id=1, source_target_pairs={{30,0},{0,2},{2,4},{4,6},{6,8},{8,10},{10,12},{12,14},{14,16},{16,... | collective-permute-start | bytes 49160 | tf_op jit(solution)/shard_map/while/body/eval_jaxpr/ppermute | solution.py:13
  279.4 6.4 %collective-permute-start.1 = (f32[64,256]{1,0:T(8,128)S(1)}, f32[64,256]{1,0:T(8,128)S(1)}, u32[]{:S(2)}, u32[]{:S(2)}) collective-permute-start(f32[64,256]{1,0:T(8,128)S(1)} %get-tuple-element.90), channel_id=1, source_target_pairs={{30,0},{0,2},{2,4},{4,6},{6,8},{8,10},{10,12},{12,14},{14,16},{16,... | collective-permute-start | bytes 196616 | tf_op jit(solution)/shard_map/while/body/eval_jaxpr/ppermute | solution.py:13
  280.0 7.7 %collective-permute-start = (f32[64,640]{1,0:T(8,128)S(1)}, f32[64,640]{1,0:T(8,128)S(1)}, u32[]{:S(2)}, u32[]{:S(2)}) collective-permute-start(f32[64,640]{1,0:T(8,128)S(1)} %get-tuple-element.88), channel_id=1, source_target_pairs={{30,0},{0,2},{2,4},{4,6},{6,8},{8,10},{10,12},{12,14},{14,16},{16,... | collective-permute-start | bytes 491528 | tf_op jit(solution)/shard_map/while/body/eval_jaxpr/ppermute | solution.py:13
  280.7 7.3 %collective-permute-start.2 = (f32[64,64]{1,0:T(8,128)S(1)}, f32[64,64]{1,0:T(8,128)S(1)}, u32[]{:S(2)}, u32[]{:S(2)}) collective-permute-start(f32[64,64]{1,0:T(8,128)S(1)} %get-tuple-element.93), channel_id=1, source_target_pairs={{30,0},{0,2},{2,4},{4,6},{6,8},{8,10},{10,12},{12,14},{14,16},{16,... | collective-permute-start | bytes 49160 | tf_op jit(solution)/shard_map/while/body/eval_jaxpr/ppermute | solution.py:13
  335.0 6.4 %collective-permute-start.1 = (f32[64,256]{1,0:T(8,128)S(1)}, f32[64,256]{1,0:T(8,128)S(1)}, u32[]{:S(2)}, u32[]{:S(2)}) collective-permute-start(f32[64,256]{1,0:T(8,128)S(1)} %get-tuple-element.90), channel_id=1, source_target_pairs={{30,0},{0,2},{2,4},{4,6},{6,8},{8,10},{10,12},{12,14},{14,16},{16,... | collective-permute-start | bytes 196616 | tf_op jit(solution)/shard_map/while/body/eval_jaxpr/ppermute | solution.py:13
  335.6 7.7 %collective-permute-start = (f32[64,640]{1,0:T(8,128)S(1)}, f32[64,640]{1,0:T(8,128)S(1)}, u32[]{:S(2)}, u32[]{:S(2)}) collective-permute-start(f32[64,640]{1,0:T(8,128)S(1)} %get-tuple-element.88), channel_id=1, source_target_pairs={{30,0},{0,2},{2,4},{4,6},{6,8},{8,10},{10,12},{12,14},{14,16},{16,... | collective-permute-start | bytes 491528 | tf_op jit(solution)/shard_map/while/body/eval_jaxpr/ppermute | solution.py:13
  336.3 7.3 %collective-permute-start.2 = (f32[64,64]{1,0:T(8,128)S(1)}, f32[64,64]{1,0:T(8,128)S(1)}, u32[]{:S(2)}, u32[]{:S(2)}) collective-permute-start(f32[64,64]{1,0:T(8,128)S(1)} %get-tuple-element.93), channel_id=1, source_target_pairs={{30,0},{0,2},{2,4},{4,6},{6,8},{8,10},{10,12},{12,14},{14,16},{16,... | collective-permute-start | bytes 49160 | tf_op jit(solution)/shard_map/while/body/eval_jaxpr/ppermute | solution.py:13
  343.6 0.7 copy-start
  343.6 0.8 copy-start.1
where the time goes:
time: 345 us; the launch traced here: 344 us
  other arithmetic  213 us (62%)
  blocking collectives  57.1 us (17%)
  waiting for transfers between devices  42.3 us (12%)
  matrix products  23.3 us (7%)
  local copies, waits for them, and re-layouts  4.8 us (1%)
    another operation x18, other arithmetic, rotation(): jnp.linalg.cholesky(jnp.dot(first.T, first, precision=HIGHEST_PREC))  74.8 us
    another operation x18, other arithmetic, rotation(): jnp.linalg.cholesky(jnp.dot(pair_gram, pair_gram, precision=HIGHEST_PREC))  74.3 us
    another operation x12, other arithmetic, rotation(): return jax.scipy.linalg.solve_triangular(second, first.T, lower=True).T  63.1 us
    psum x6, blocking collectives, advance_cross(): lax.psum(gram_of(column_pair[:block_width], column_pair[block_width:]), '...  46.7 us
    ppermute x18, waiting for transfers between devices, shifted(): return lax.ppermute(block, axis, route)  42.3 us
    psum x1, blocking collectives, body(): lax.psum((gram_of(columns[:block_width], columns[:block_width]), gram_of(...  10.4 us
  transfers between devices with their start and end apart: 18, of which 18 were waited for; matrix products, arithmetic and copies ran while one was open for 2% of the time, Pallas kernels for 0%

commit v1 on v0

--- a/solution.py
+++ b/solution.py
@@ -41,7 +41,10 @@
 
     def advance_cross(step_index, loop_state):
         column_pair, factor_pair, stay_gram, moving_gram = loop_state
-        cross_term = lax.psum(gram_of(column_pair[:block_width], column_pair[block_width:]), "rows")
+        cross_term = jnp.sum(
+            lax.all_gather(gram_of(column_pair[:block_width], column_pair[block_width:]), "rows"),
+            axis=0,
+        )
         upper_half = jnp.concatenate([stay_gram, cross_term], 1)
         lower_half = jnp.concatenate([cross_term.T, moving_gram], 1)
         pair_gram = jnp.concatenate([upper_half, lower_half], 0)

time: 345 us -> 324 us (0.939)
  blocking collectives: 57.1 us -> 37.9 us
    psum x6 -> x0, blocking collectives: 46.7 us -> none  [advance_cross(): lax.psum(gram_of(column_pair[:block_width], column_pair[block_width:]), '...]
    all_gather x0 -> x6, blocking collectives: none -> 27.5 us  [advance_cross(): lax.all_gather(gram_of(column_pair[:block_width], column_pair[block_width...]
where the time goes in v1:
time: 324 us; the launch traced here: 323 us
  other arithmetic  213 us (66%)
  waiting for transfers between devices  42.5 us (13%)
  blocking collectives  37.9 us (12%)
  matrix products  22.4 us (7%)
  local copies, waits for them, and re-layouts  3.9 us (1%)
    another operation x18, other arithmetic, rotation(): jnp.linalg.cholesky(jnp.dot(first.T, first, precision=HIGHEST_PREC))  74.8 us
    another operation x18, other arithmetic, rotation(): jnp.linalg.cholesky(jnp.dot(pair_gram, pair_gram, precision=HIGHEST_PREC))  74.3 us
    another operation x12, other arithmetic, rotation(): return jax.scipy.linalg.solve_triangular(second, first.T, lower=True).T  63.1 us
    ppermute x18, waiting for transfers between devices, shifted(): return lax.ppermute(block, axis, route)  42.5 us
    all_gather x6, blocking collectives, advance_cross(): lax.all_gather(gram_of(column_pair[:block_width], column_pair[block_width...  27.5 us
    psum x1, blocking collectives, body(): lax.psum((gram_of(columns[:block_width], columns[:block_width]), gram_of(...  10.4 us
  transfers between devices with their start and end apart: 18, of which 18 were waited for; matrix products, arithmetic and copies ran while one was open for 2% of the time, Pallas kernels for 0%

profile of v1, /device:TPU:0, one launch (start us, length us, event | category | flops | bytes accessed | tf_op | source)
XLA Modules:
  0.0 323.2 jit_solution(8555355982239525635)
XLA Ops:
  0.6 1.0 copy.31
  2.2 10.4 %all-reduce = (f32[64,64]{1,0:T(8,128)S(1)}, f32[64,64]{1,0:T(8,128)S(1)}) all-reduce(f32[64,64]{1,0:T(8,128)S(1)} %fusion.27, f32[64,64]{1,0:T(8,128)S(1)} %fusion.25), channel_id=1, replica_groups=mesh['blk'=16,'rows'=2] {'rows'}, use_global_device_ids=true, to_apply=%region_0.0 | all-reduce | flops 8192 | bytes 65536 | tf_op jit(solution)/shard_map/psum | solution.py:34
  12.7 309.7 %while.16 = (s32[]{:T(128)}, f32[128,640]{1,0:T(8,128)S(1)}, f32[128,256]{1,0:T(8,128)S(1)}, f32[64,64]{1,0:T(8,128)S(1)}, f32[64,64]{1,0:T(8,128)S(1)}, /*index=5*/s32[]{:T(128)}, f32[]{:T(128)}) while((s32[]{:T(128)}, f32[128,640]{1,0:T(8,128)S(1)}, f32[128,256]{1,0:T(8,128)S(1)}, f32[64,64]{1,0:T(8,128)S(1)}, f32[64,64]{1,0:T(8,128)S(1)}, ...), condition=%wide.region_6.8_spmd, body=%wide.region_2.7_spmd.sunk | while | flops 333992192 | bytes 6179022 | solution.py:73
  13.0 4.6 %all-gather.2 = f32[128,64]{1,0:T(8,128)S(1)} all-gather(f32[64,64]{1,0:T(8,128)S(1)} %fusion.77), channel_id=2, replica_groups=mesh['blk'=16,'rows'=2] {'rows'}, dimensions={0}, use_global_device_ids=true | all-gather | bytes 49152 | tf_op jit(solution)/shard_map/while/body/eval_jaxpr/all_gather | solution.py:45
  18.1 11.7 %cholesky.175 = f32[128,128]{1,0:T(8,128)S(1)} custom-call(f32[128,128]{1,0:T(8,128)S(1)} %fusion.79), custom_call_target="Cholesky" | custom-call | tf_op jit(solution)/shard_map/while/body/eval_jaxpr/jit(cholesky)/cholesky | solution.py:17
  30.5 0.9 fusion.81
  31.5 11.7 %cholesky.176 = f32[128,128]{1,0:T(8,128)S(1)} custom-call(f32[128,128]{1,0:T(8,128)S(1)} %fusion.82), custom_call_target="Cholesky" | custom-call | tf_op jit(solution)/shard_map/while/body/eval_jaxpr/jit(cholesky)/cholesky | solution.py:18
  43.3 0.7 compare_reduce_fusion.5
  44.0 0.7 fusion.83
  44.7 9.8 %custom-call.7 = f32[1,128,128]{1,2,0:T(8,128)S(1)} custom-call(f32[1,128,128]{2,1,0:T(8,128)S(1)} %fusion.83), custom_call_target="InvertDiagBlocksLowerTriangular" | custom-call | tf_op jit(solution)/shard_map/while/body/eval_jaxpr/jit(_solve_triangular)/triangular_solve | solution.py:19
  54.5 0.9 fusion.84
  56.3 1.5 collective-permute-start
  58.4 3.8 %collective-permute-done.1 = f32[64,256]{1,0:T(8,128)S(1)} collective-permute-done((f32[64,256]{1,0:T(8,128)S(1)}, f32[64,256]{1,0:T(8,128)S(1)}, u32[]{:S(2)}, u32[]{:S(2)}) %collective-permute-start.1) | collective-permute-done | bytes 65568 | tf_op jit(solution)/shard_map/while/body/eval_jaxpr/ppermute | solution.py:13
  62.2 1.7 collective-permute-done
  64.7 4.6 %all-gather.2 = f32[128,64]{1,0:T(8,128)S(1)} all-gather(f32[64,64]{1,0:T(8,128)S(1)} %fusion.77), channel_id=2, replica_groups=mesh['blk'=16,'rows'=2] {'rows'}, dimensions={0}, use_global_device_ids=true | all-gather | bytes 49152 | tf_op jit(solution)/shard_map/while/body/eval_jaxpr/all_gather | solution.py:45
  69.8 11.7 %cholesky.175 = f32[128,128]{1,0:T(8,128)S(1)} custom-call(f32[128,128]{1,0:T(8,128)S(1)} %fusion.79), custom_call_target="Cholesky" | custom-call | tf_op jit(solution)/shard_map/while/body/eval_jaxpr/jit(cholesky)/cholesky | solution.py:17
  82.2 0.9 fusion.81
  83.3 11.7 %cholesky.176 = f32[128,128]{1,0:T(8,128)S(1)} custom-call(f32[128,128]{1,0:T(8,128)S(1)} %fusion.82), custom_call_target="Cholesky" | custom-call | tf_op jit(solution)/shard_map/while/body/eval_jaxpr/jit(cholesky)/cholesky | solution.py:18
  95.0 0.7 compare_reduce_fusion.5
  95.7 0.7 fusion.83
  96.4 9.8 %custom-call.7 = f32[1,128,128]{1,2,0:T(8,128)S(1)} custom-call(f32[1,128,128]{2,1,0:T(8,128)S(1)} %fusion.83), custom_call_target="InvertDiagBlocksLowerTriangular" | custom-call | tf_op jit(solution)/shard_map/while/body/eval_jaxpr/jit(_solve_triangular)/triangular_solve | solution.py:19
  106.2 0.9 fusion.84
  108.7 5.2 %collective-permute-done.1 = f32[64,256]{1,0:T(8,128)S(1)} collective-permute-done((f32[64,256]{1,0:T(8,128)S(1)}, f32[64,256]{1,0:T(8,128)S(1)}, u32[]{:S(2)}, u32[]{:S(2)}) %collective-permute-start.1) | collective-permute-done | bytes 65568 | tf_op jit(solution)/shard_map/while/body/eval_jaxpr/ppermute | solution.py:13
  113.9 1.7 collective-permute-done
  116.3 4.6 %all-gather.2 = f32[128,64]{1,0:T(8,128)S(1)} all-gather(f32[64,64]{1,0:T(8,128)S(1)} %fusion.77), channel_id=2, replica_groups=mesh['blk'=16,'rows'=2] {'rows'}, dimensions={0}, use_global_device_ids=true | all-gather | bytes 49152 | tf_op jit(solution)/shard_map/while/body/eval_jaxpr/all_gather | solution.py:45
  121.4 11.7 %cholesky.175 = f32[128,128]{1,0:T(8,128)S(1)} custom-call(f32[128,128]{1,0:T(8,128)S(1)} %fusion.79), custom_call_target="Cholesky" | custom-call | tf_op jit(solution)/shard_map/while/body/eval_jaxpr/jit(cholesky)/cholesky | solution.py:17
  133.8 0.9 fusion.81
  134.9 11.7 %cholesky.176 = f32[128,128]{1,0:T(8,128)S(1)} custom-call(f32[128,128]{1,0:T(8,128)S(1)} %fusion.82), custom_call_target="Cholesky" | custom-call | tf_op jit(solution)/shard_map/while/body/eval_jaxpr/jit(cholesky)/cholesky | solution.py:18
  146.6 0.7 compare_reduce_fusion.5
  147.3 0.7 fusion.83
  148.0 9.8 %custom-call.7 = f32[1,128,128]{1,2,0:T(8,128)S(1)} custom-call(f32[1,128,128]{2,1,0:T(8,128)S(1)} %fusion.83), custom_call_target="InvertDiagBlocksLowerTriangular" | custom-call | tf_op jit(solution)/shard_map/while/body/eval_jaxpr/jit(_solve_triangular)/triangular_solve | solution.py:19
  157.8 0.9 fusion.84
  160.3 5.2 %collective-permute-done.1 = f32[64,256]{1,0:T(8,128)S(1)} collective-permute-done((f32[64,256]{1,0:T(8,128)S(1)}, f32[64,256]{1,0:T(8,128)S(1)}, u32[]{:S(2)}, u32[]{:S(2)}) %collective-permute-start.1) | collective-permute-done | bytes 65568 | tf_op jit(solution)/shard_map/while/body/eval_jaxpr/ppermute | solution.py:13
  165.5 1.7 collective-permute-done
  167.9 4.6 %all-gather.2 = f32[128,64]{1,0:T(8,128)S(1)} all-gather(f32[64,64]{1,0:T(8,128)S(1)} %fusion.77), channel_id=2, replica_groups=mesh['blk'=16,'rows'=2] {'rows'}, dimensions={0}, use_global_device_ids=true | all-gather | bytes 49152 | tf_op jit(solution)/shard_map/while/body/eval_jaxpr/all_gather | solution.py:45
  173.0 11.7 %cholesky.175 = f32[128,128]{1,0:T(8,128)S(1)} custom-call(f32[128,128]{1,0:T(8,128)S(1)} %fusion.79), custom_call_target="Cholesky" | custom-call | tf_op jit(solution)/shard_map/while/body/eval_jaxpr/jit(cholesky)/cholesky | solution.py:17
  185.4 0.9 fusion.81
  186.4 11.7 %cholesky.176 = f32[128,128]{1,0:T(8,128)S(1)} custom-call(f32[128,128]{1,0:T(8,128)S(1)} %fusion.82), custom_call_target="Cholesky" | custom-call | tf_op jit(solution)/shard_map/while/body/eval_jaxpr/jit(cholesky)/cholesky | solution.py:18
  198.2 0.7 compare_reduce_fusion.5
  198.9 0.7 fusion.83
  199.6 9.8 %custom-call.7 = f32[1,128,128]{1,2,0:T(8,128)S(1)} custom-call(f32[1,128,128]{2,1,0:T(8,128)S(1)} %fusion.83), custom_call_target="InvertDiagBlocksLowerTriangular" | custom-call | tf_op jit(solution)/shard_map/while/body/eval_jaxpr/jit(_solve_triangular)/triangular_solve | solution.py:19
  209.4 0.9 fusion.84
  211.9 5.2 %collective-permute-done.1 = f32[64,256]{1,0:T(8,128)S(1)} collective-permute-done((f32[64,256]{1,0:T(8,128)S(1)}, f32[64,256]{1,0:T(8,128)S(1)}, u32[]{:S(2)}, u32[]{:S(2)}) %collective-permute-start.1) | collective-permute-done | bytes 65568 | tf_op jit(solution)/shard_map/while/body/eval_jaxpr/ppermute | solution.py:13
  217.1 1.7 collective-permute-done
  219.5 4.6 %all-gather.2 = f32[128,64]{1,0:T(8,128)S(1)} all-gather(f32[64,64]{1,0:T(8,128)S(1)} %fusion.77), channel_id=2, replica_groups=mesh['blk'=16,'rows'=2] {'rows'}, dimensions={0}, use_global_device_ids=true | all-gather | bytes 49152 | tf_op jit(solution)/shard_map/while/body/eval_jaxpr/all_gather | solution.py:45
  224.6 11.7 %cholesky.175 = f32[128,128]{1,0:T(8,128)S(1)} custom-call(f32[128,128]{1,0:T(8,128)S(1)} %fusion.79), custom_call_target="Cholesky" | custom-call | tf_op jit(solution)/shard_map/while/body/eval_jaxpr/jit(cholesky)/cholesky | solution.py:17
  237.0 0.9 fusion.81
  238.0 11.7 %cholesky.176 = f32[128,128]{1,0:T(8,128)S(1)} custom-call(f32[128,128]{1,0:T(8,128)S(1)} %fusion.82), custom_call_target="Cholesky" | custom-call | tf_op jit(solution)/shard_map/while/body/eval_jaxpr/jit(cholesky)/cholesky | solution.py:18
  249.8 0.7 compare_reduce_fusion.5
  250.5 0.7 fusion.83
  251.2 9.8 %custom-call.7 = f32[1,128,128]{1,2,0:T(8,128)S(1)} custom-call(f32[1,128,128]{2,1,0:T(8,128)S(1)} %fusion.83), custom_call_target="InvertDiagBlocksLowerTriangular" | custom-call | tf_op jit(solution)/shard_map/while/body/eval_jaxpr/jit(_solve_triangular)/triangular_solve | solution.py:19
  261.0 0.9 fusion.84
  263.5 5.2 %collective-permute-done.1 = f32[64,256]{1,0:T(8,128)S(1)} collective-permute-done((f32[64,256]{1,0:T(8,128)S(1)}, f32[64,256]{1,0:T(8,128)S(1)}, u32[]{:S(2)}, u32[]{:S(2)}) %collective-permute-start.1) | collective-permute-done | bytes 65568 | tf_op jit(solution)/shard_map/while/body/eval_jaxpr/ppermute | solution.py:13
  268.7 1.7 collective-permute-done
  271.1 4.6 %all-gather.2 = f32[128,64]{1,0:T(8,128)S(1)} all-gather(f32[64,64]{1,0:T(8,128)S(1)} %fusion.77), channel_id=2, replica_groups=mesh['blk'=16,'rows'=2] {'rows'}, dimensions={0}, use_global_device_ids=true | all-gather | bytes 49152 | tf_op jit(solution)/shard_map/while/body/eval_jaxpr/all_gather | solution.py:45
  276.2 11.7 %cholesky.175 = f32[128,128]{1,0:T(8,128)S(1)} custom-call(f32[128,128]{1,0:T(8,128)S(1)} %fusion.79), custom_call_target="Cholesky" | custom-call | tf_op jit(solution)/shard_map/while/body/eval_jaxpr/jit(cholesky)/cholesky | solution.py:17
  288.6 0.9 fusion.81
  289.6 11.7 %cholesky.176 = f32[128,128]{1,0:T(8,128)S(1)} custom-call(f32[128,128]{1,0:T(8,128)S(1)} %fusion.82), custom_call_target="Cholesky" | custom-call | tf_op jit(solution)/shard_map/while/body/eval_jaxpr/jit(cholesky)/cholesky | solution.py:18
  301.4 0.7 compare_reduce_fusion.5
  302.8 9.8 %custom-call.7 = f32[1,128,128]{1,2,0:T(8,128)S(1)} custom-call(f32[1,128,128]{2,1,0:T(8,128)S(1)} %fusion.83), custom_call_target="InvertDiagBlocksLowerTriangular" | custom-call | tf_op jit(solution)/shard_map/while/body/eval_jaxpr/jit(_solve_triangular)/triangular_solve | solution.py:19
  312.6 0.9 fusion.84
  315.1 5.2 %collective-permute-done.1 = f32[64,256]{1,0:T(8,128)S(1)} collective-permute-done((f32[64,256]{1,0:T(8,128)S(1)}, f32[64,256]{1,0:T(8,128)S(1)}, u32[]{:S(2)}, u32[]{:S(2)}) %collective-permute-start.1) | collective-permute-done | bytes 65568 | tf_op jit(solution)/shard_map/while/body/eval_jaxpr/ppermute | solution.py:13
  320.3 1.7 collective-permute-done
  322.4 0.7 copy-done
  (151 shorter events, 21.6 us)
Async XLA Ops:
  1.9 10.8 %copy-start.2 = (f32[128,256]{1,0:T(8,128)S(1)}, f32[128,256]{1,0:T(8,128)}, u32[]{:S(2)}) copy-start(f32[128,256]{1,0:T(8,128)} %param.6) | copy-start | bytes 393220
  55.7 6.4 %collective-permute-start.1 = (f32[64,256]{1,0:T(8,128)S(1)}, f32[64,256]{1,0:T(8,128)S(1)}, u32[]{:S(2)}, u32[]{:S(2)}) collective-permute-start(f32[64,256]{1,0:T(8,128)S(1)} %get-tuple-element.90), channel_id=1, source_target_pairs={{30,0},{0,2},{2,4},{4,6},{6,8},{8,10},{10,12},{12,14},{14,16},{16,... | collective-permute-start | bytes 196616 | tf_op jit(solution)/shard_map/while/body/eval_jaxpr/ppermute | solution.py:13
  56.3 7.7 %collective-permute-start = (f32[64,640]{1,0:T(8,128)S(1)}, f32[64,640]{1,0:T(8,128)S(1)}, u32[]{:S(2)}, u32[]{:S(2)}) collective-permute-start(f32[64,640]{1,0:T(8,128)S(1)} %get-tuple-element.88), channel_id=1, source_target_pairs={{30,0},{0,2},{2,4},{4,6},{6,8},{8,10},{10,12},{12,14},{14,16},{16,... | collective-permute-start | bytes 491528 | tf_op jit(solution)/shard_map/while/body/eval_jaxpr/ppermute | solution.py:13
  58.4 6.0 %collective-permute-start.2 = (f32[64,64]{1,0:T(8,128)S(1)}, f32[64,64]{1,0:T(8,128)S(1)}, u32[]{:S(2)}, u32[]{:S(2)}) collective-permute-start(f32[64,64]{1,0:T(8,128)S(1)} %get-tuple-element.93), channel_id=1, source_target_pairs={{30,0},{0,2},{2,4},{4,6},{6,8},{8,10},{10,12},{12,14},{14,16},{16,... | collective-permute-start | bytes 49160 | tf_op jit(solution)/shard_map/while/body/eval_jaxpr/ppermute | solution.py:13
  107.5 6.4 %collective-permute-start.1 = (f32[64,256]{1,0:T(8,128)S(1)}, f32[64,256]{1,0:T(8,128)S(1)}, u32[]{:S(2)}, u32[]{:S(2)}) collective-permute-start(f32[64,256]{1,0:T(8,128)S(1)} %get-tuple-element.90), channel_id=1, source_target_pairs={{30,0},{0,2},{2,4},{4,6},{6,8},{8,10},{10,12},{12,14},{14,16},{16,... | collective-permute-start | bytes 196616 | tf_op jit(solution)/shard_map/while/body/eval_jaxpr/ppermute | solution.py:13
  108.0 7.7 %collective-permute-start = (f32[64,640]{1,0:T(8,128)S(1)}, f32[64,640]{1,0:T(8,128)S(1)}, u32[]{:S(2)}, u32[]{:S(2)}) collective-permute-start(f32[64,640]{1,0:T(8,128)S(1)} %get-tuple-element.88), channel_id=1, source_target_pairs={{30,0},{0,2},{2,4},{4,6},{6,8},{8,10},{10,12},{12,14},{14,16},{16,... | collective-permute-start | bytes 491528 | tf_op jit(solution)/shard_map/while/body/eval_jaxpr/ppermute | solution.py:13
  108.7 7.4 %collective-permute-start.2 = (f32[64,64]{1,0:T(8,128)S(1)}, f32[64,64]{1,0:T(8,128)S(1)}, u32[]{:S(2)}, u32[]{:S(2)}) collective-permute-start(f32[64,64]{1,0:T(8,128)S(1)} %get-tuple-element.93), channel_id=1, source_target_pairs={{30,0},{0,2},{2,4},{4,6},{6,8},{8,10},{10,12},{12,14},{14,16},{16,... | collective-permute-start | bytes 49160 | tf_op jit(solution)/shard_map/while/body/eval_jaxpr/ppermute | solution.py:13
  159.1 6.4 %collective-permute-start.1 = (f32[64,256]{1,0:T(8,128)S(1)}, f32[64,256]{1,0:T(8,128)S(1)}, u32[]{:S(2)}, u32[]{:S(2)}) collective-permute-start(f32[64,256]{1,0:T(8,128)S(1)} %get-tuple-element.90), channel_id=1, source_target_pairs={{30,0},{0,2},{2,4},{4,6},{6,8},{8,10},{10,12},{12,14},{14,16},{16,... | collective-permute-start | bytes 196616 | tf_op jit(solution)/shard_map/while/body/eval_jaxpr/ppermute | solution.py:13
  159.6 7.7 %collective-permute-start = (f32[64,640]{1,0:T(8,128)S(1)}, f32[64,640]{1,0:T(8,128)S(1)}, u32[]{:S(2)}, u32[]{:S(2)}) collective-permute-start(f32[64,640]{1,0:T(8,128)S(1)} %get-tuple-element.88), channel_id=1, source_target_pairs={{30,0},{0,2},{2,4},{4,6},{6,8},{8,10},{10,12},{12,14},{14,16},{16,... | collective-permute-start | bytes 491528 | tf_op jit(solution)/shard_map/while/body/eval_jaxpr/ppermute | solution.py:13
  160.3 7.4 %collective-permute-start.2 = (f32[64,64]{1,0:T(8,128)S(1)}, f32[64,64]{1,0:T(8,128)S(1)}, u32[]{:S(2)}, u32[]{:S(2)}) collective-permute-start(f32[64,64]{1,0:T(8,128)S(1)} %get-tuple-element.93), channel_id=1, source_target_pairs={{30,0},{0,2},{2,4},{4,6},{6,8},{8,10},{10,12},{12,14},{14,16},{16,... | collective-permute-start | bytes 49160 | tf_op jit(solution)/shard_map/while/body/eval_jaxpr/ppermute | solution.py:13
  210.7 6.4 %collective-permute-start.1 = (f32[64,256]{1,0:T(8,128)S(1)}, f32[64,256]{1,0:T(8,128)S(1)}, u32[]{:S(2)}, u32[]{:S(2)}) collective-permute-start(f32[64,256]{1,0:T(8,128)S(1)} %get-tuple-element.90), channel_id=1, source_target_pairs={{30,0},{0,2},{2,4},{4,6},{6,8},{8,10},{10,12},{12,14},{14,16},{16,... | collective-permute-start | bytes 196616 | tf_op jit(solution)/shard_map/while/body/eval_jaxpr/ppermute | solution.py:13
  211.2 7.7 %collective-permute-start = (f32[64,640]{1,0:T(8,128)S(1)}, f32[64,640]{1,0:T(8,128)S(1)}, u32[]{:S(2)}, u32[]{:S(2)}) collective-permute-start(f32[64,640]{1,0:T(8,128)S(1)} %get-tuple-element.88), channel_id=1, source_target_pairs={{30,0},{0,2},{2,4},{4,6},{6,8},{8,10},{10,12},{12,14},{14,16},{16,... | collective-permute-start | bytes 491528 | tf_op jit(solution)/shard_map/while/body/eval_jaxpr/ppermute | solution.py:13
  211.9 7.4 %collective-permute-start.2 = (f32[64,64]{1,0:T(8,128)S(1)}, f32[64,64]{1,0:T(8,128)S(1)}, u32[]{:S(2)}, u32[]{:S(2)}) collective-permute-start(f32[64,64]{1,0:T(8,128)S(1)} %get-tuple-element.93), channel_id=1, source_target_pairs={{30,0},{0,2},{2,4},{4,6},{6,8},{8,10},{10,12},{12,14},{14,16},{16,... | collective-permute-start | bytes 49160 | tf_op jit(solution)/shard_map/while/body/eval_jaxpr/ppermute | solution.py:13
  262.3 6.4 %collective-permute-start.1 = (f32[64,256]{1,0:T(8,128)S(1)}, f32[64,256]{1,0:T(8,128)S(1)}, u32[]{:S(2)}, u32[]{:S(2)}) collective-permute-start(f32[64,256]{1,0:T(8,128)S(1)} %get-tuple-element.90), channel_id=1, source_target_pairs={{30,0},{0,2},{2,4},{4,6},{6,8},{8,10},{10,12},{12,14},{14,16},{16,... | collective-permute-start | bytes 196616 | tf_op jit(solution)/shard_map/while/body/eval_jaxpr/ppermute | solution.py:13
  262.8 7.7 %collective-permute-start = (f32[64,640]{1,0:T(8,128)S(1)}, f32[64,640]{1,0:T(8,128)S(1)}, u32[]{:S(2)}, u32[]{:S(2)}) collective-permute-start(f32[64,640]{1,0:T(8,128)S(1)} %get-tuple-element.88), channel_id=1, source_target_pairs={{30,0},{0,2},{2,4},{4,6},{6,8},{8,10},{10,12},{12,14},{14,16},{16,... | collective-permute-start | bytes 491528 | tf_op jit(solution)/shard_map/while/body/eval_jaxpr/ppermute | solution.py:13
  263.4 7.4 %collective-permute-start.2 = (f32[64,64]{1,0:T(8,128)S(1)}, f32[64,64]{1,0:T(8,128)S(1)}, u32[]{:S(2)}, u32[]{:S(2)}) collective-permute-start(f32[64,64]{1,0:T(8,128)S(1)} %get-tuple-element.93), channel_id=1, source_target_pairs={{30,0},{0,2},{2,4},{4,6},{6,8},{8,10},{10,12},{12,14},{14,16},{16,... | collective-permute-start | bytes 49160 | tf_op jit(solution)/shard_map/while/body/eval_jaxpr/ppermute | solution.py:13
  313.9 6.4 %collective-permute-start.1 = (f32[64,256]{1,0:T(8,128)S(1)}, f32[64,256]{1,0:T(8,128)S(1)}, u32[]{:S(2)}, u32[]{:S(2)}) collective-permute-start(f32[64,256]{1,0:T(8,128)S(1)} %get-tuple-element.90), channel_id=1, source_target_pairs={{30,0},{0,2},{2,4},{4,6},{6,8},{8,10},{10,12},{12,14},{14,16},{16,... | collective-permute-start | bytes 196616 | tf_op jit(solution)/shard_map/while/body/eval_jaxpr/ppermute | solution.py:13
  314.4 7.7 %collective-permute-start = (f32[64,640]{1,0:T(8,128)S(1)}, f32[64,640]{1,0:T(8,128)S(1)}, u32[]{:S(2)}, u32[]{:S(2)}) collective-permute-start(f32[64,640]{1,0:T(8,128)S(1)} %get-tuple-element.88), channel_id=1, source_target_pairs={{30,0},{0,2},{2,4},{4,6},{6,8},{8,10},{10,12},{12,14},{14,16},{16,... | collective-permute-start | bytes 491528 | tf_op jit(solution)/shard_map/while/body/eval_jaxpr/ppermute | solution.py:13
  315.0 7.4 %collective-permute-start.2 = (f32[64,64]{1,0:T(8,128)S(1)}, f32[64,64]{1,0:T(8,128)S(1)}, u32[]{:S(2)}, u32[]{:S(2)}) collective-permute-start(f32[64,64]{1,0:T(8,128)S(1)} %get-tuple-element.93), channel_id=1, source_target_pairs={{30,0},{0,2},{2,4},{4,6},{6,8},{8,10},{10,12},{12,14},{14,16},{16,... | collective-permute-start | bytes 49160 | tf_op jit(solution)/shard_map/while/body/eval_jaxpr/ppermute | solution.py:13
  322.4 0.7 copy-start
  322.4 0.8 copy-start.1
